TPU v7x, 32 devices: a whole 2x2x4 slice. The times are simulated.
32 devices in a mesh: day: 2 (over x), chan: 16 (over z, y, core).
Axes of the slice: x: 2, y: 2, z: 4, core: 2. Of those that a mesh axis runs over, the one named last changes fastest.
Arguments:
- file_blocks: bfloat16 [224, 16, 1024], P(('day', 'chan')), parts along dimension 0, may hold values from -132 to 132
- block_target: int32 [224], P(('day', 'chan')), parts along dimension 0, may hold values from -1 to 63, as said below
Outputs:
- correlations: bfloat16 [512, 64, 144], P(('day', 'chan')), parts along dimension 0
There are 2 independent parts, one for each index of `day`. A program takes and returns all parts, laid end to end along the dimension named above; each array names one. Nothing has to cross between parts.
Inputs may be any that keep to these rules, and one draw needn't show every extreme that they name: `block_target`: -1 marks an empty slot and a device's filled slots come first; each device holds 1 to 7 blocks. A value v names window v % 4 of channel owner v // 4; every such pair appears exactly once. Devices 2k and 2k+1 together hold exactly the 8 blocks of owners 2k and 2k+1; in every draw some device holds all 4 blocks of its neighbour owner in the pair.
All inputs are finite; a program needn't handle non-finite values.
Results may differ from a plain program's by a relative error of at most 0.0073.
Values may be sent and summed in bfloat16 or wider, within the bound.
A program may use at most 64 MiB of HBM per device.

v0:
```python
import math

import jax
import jax.numpy as jnp
from jax import lax
from jax.sharding import PartitionSpec as P

NW = 4
BANDS = 128
BAND_LO = 16
SMOOTH = 4
LAGS = 64


def swapped(block, axis, apart):
    count = lax.axis_size(axis)
    route = []
    for low in range(count):
        high = low | 1 << apart
        if high != low and high < count:
            route += [(low, high), (high, low)]
    return lax.ppermute(block, axis, route)


def from_behind(value, axis, steps):
    count = lax.axis_size(axis)
    pairs = [(source, (source + steps) % count) for source in range(count)]
    return lax.ppermute(value, axis, pairs)


def fourier_table(samples, bands, band_low):
    times = jnp.arange(samples, dtype=jnp.int32)
    bins = band_low + jnp.arange(bands, dtype=jnp.int32)
    phase = times[:, None] * bins[None, :] % samples
    angle = 2.0 * math.pi / samples * phase.astype(jnp.float32)
    taper = 0.5 - 0.5 * jnp.cos(2.0 * math.pi / samples * times.astype(jnp.float32))
    rows = jnp.concatenate(
        [taper[:, None] * jnp.cos(angle), -taper[:, None] * jnp.sin(angle)], axis=1
    )
    return rows.astype(jnp.bfloat16)


def lag_table(samples, bands, band_low, lags, windows):
    bins = band_low + jnp.arange(bands, dtype=jnp.int32)
    delays = jnp.arange(lags, dtype=jnp.int32) - lags // 2
    phase = bins[:, None] * delays[None, :] % samples
    angle = 2.0 * math.pi / samples * phase.astype(jnp.float32)
    weight = 1.0 / math.sqrt(windows * bands)
    rows = jnp.stack([jnp.cos(angle) * weight, -jnp.sin(angle) * weight])
    return rows.astype(jnp.bfloat16)


def whiten(spectra, bands, smooth):
    real_part = spectra[..., :bands]
    imag_part = spectra[..., bands:]
    power = real_part * real_part + imag_part * imag_part
    widths = [(0, 0)] * (power.ndim - 1) + [(smooth, smooth)]
    padded = jnp.pad(power, widths)
    nearby = padded[..., 0:bands]
    for shift_bins in range(1, 2 * smooth + 1):
        nearby = nearby + padded[..., shift_bins : shift_bins + bands]
    level = nearby / (2 * smooth + 1) + 0.25 * jnp.mean(power, axis=-1, keepdims=True) + 1e-05
    factor = lax.rsqrt(level)
    return jnp.concatenate([real_part * factor, imag_part * factor], axis=-1).astype(jnp.bfloat16)


def pair_cross(own_block, other_block, bands):
    windows = own_block.shape[0]
    own_split = own_block.reshape(windows, own_block.shape[1], 2, bands)
    other_split = other_block.reshape(windows, other_block.shape[1], 2, bands)
    same_part = jnp.einsum(
        "wicb,wjcb->bij", own_split, other_split, preferred_element_type=jnp.float32
    )
    turned = jnp.einsum(
        "wib,wjb->bij", own_split[:, :, 1], other_split[:, :, 0], preferred_element_type=jnp.float32
    )
    turned = turned - jnp.einsum(
        "wib,wjb->bij", own_split[:, :, 0], other_split[:, :, 1], preferred_element_type=jnp.float32
    )
    return jnp.stack([same_part, turned]).astype(jnp.bfloat16)


def shards(file_blocks, block_target):
    slot_count, channels, samples = file_blocks.shape
    devices = lax.axis_size("chan")
    my_index = lax.axis_index("chan")
    partner_index = jnp.bitwise_xor(my_index, 1)
    transform = fourier_table(samples, BANDS, BAND_LO)
    lag_rows = lag_table(samples, BANDS, BAND_LO, LAGS, NW)
    filled = block_target >= 0
    owners = block_target // NW
    window_ids = block_target % NW
    wanted = jnp.arange(NW, dtype=jnp.int32)
    window_match = window_ids[None, :] == wanted[:, None]
    keep_mask = (window_match & (filled & (owners == my_index))[None, :]).astype(jnp.bfloat16)
    send_mask = (window_match & (filled & (owners == partner_index))[None, :]).astype(jnp.bfloat16)
    flat_blocks = file_blocks.reshape(slot_count, channels * samples)
    outgoing = jnp.dot(send_mask, flat_blocks, preferred_element_type=jnp.float32).astype(
        jnp.bfloat16
    )
    incoming = swapped(outgoing, "chan", 0)
    kept = jnp.dot(keep_mask, flat_blocks, preferred_element_type=jnp.float32)
    records = (kept + incoming.astype(jnp.float32)).astype(jnp.bfloat16)
    spectra = jnp.dot(
        records.reshape(NW * channels, samples), transform, preferred_element_type=jnp.float32
    )
    whitened = whiten(spectra.reshape(NW, channels, 2 * BANDS), BANDS, SMOOTH)
    half_cycle = devices // 2
    columns = (half_cycle + 1) * channels
    cross_all = jnp.zeros((2, BANDS, channels, columns), jnp.bfloat16)
    cross_all = lax.dynamic_update_slice_in_dim(
        cross_all, pair_cross(whitened, whitened, BANDS), 0, 3
    )

    def forward(step_count, cycle_state):
        moving_block, gathered = cycle_state
        moving_block = from_behind(moving_block, "chan", -1)
        pairs_now = pair_cross(whitened, moving_block, BANDS)
        gathered = lax.dynamic_update_slice_in_dim(
            gathered, pairs_now, (step_count + 1) * channels, 3
        )
        return (moving_block, gathered)

    final_state = lax.fori_loop(0, half_cycle, forward, (whitened, cross_all))
    cross_all = final_state[1]
    result = jnp.einsum("pbij,pbt->itj", cross_all, lag_rows, preferred_element_type=jnp.float32)
    return result.astype(jnp.bfloat16)


def solution(mesh):
    return jax.shard_map(
        shards,
        mesh=mesh,
        in_specs=(P(("day", "chan"), None, None), P(("day", "chan"))),
        out_specs=P(("day", "chan"), None, None),
        check_vma=False,
    )
```

profile of v0, /device:TPU:0, one launch (start us, length us, event | category | flops | bytes accessed | tf_op | source)
XLA Modules:
  0.0 80.0 jit_solution(11722908257724221265)
XLA Ops:
  0.0 0.7 and_select_fusion.1
  0.7 0.7 compare_and_fusion.1
  1.3 1.1 %copy.42 = bf16[1,7,16,1024]{3,1,2,0:T(8,128)(2,1)S(1)} copy(bf16[1,7,16,1024]{3,2,1,0:T(8,128)(2,1)} %bitcast.105) | data formatting | bytes 458752
  2.4 0.7 compare_and_fusion
  3.3 0.6 collective-permute-start.1
  3.9 2.3 %multiply_convert_fusion.1 = (bf16[1024,128]{1,0:T(8,128)(2,1)S(1)}, bf16[1024,128]{1,0:T(8,128)(2,1)S(1)}) fusion(s32[128]{0:T(128)S(1)} %iota_add_fusion.1, f32[1024]{0:T(1024)S(1)} %get-tuple-element.115, f32[1024]{0:T(1024)S(1)} %get-tuple-element.116), kind=kLoop, calls=%fused_computation.37 | loop fusion | flops 2359296 | bytes 532992 | tf_op jit(solution)/shard_map/convert.14
  7.7 0.4 fusion.10
  10.1 68.6 %while.15 = (s32[]{:T(128)}, bf16[4,16,256]{2,1,0:T(8,128)(2,1)S(1)}, bf16[2,128,16,144]{1,3,2,0:T(8,128)(2,1)S(1)}, bf16[4,16,256]{1,0,2:T(4,128)(2,1)S(1)}, s32[]{:T(128)}, /*index=5*/s32[]{:T(128)}, s32[]{:T(128)}, s32[]{:T(128)}) while((s32[]{:T(128)}, bf16[4,16,256]{2,1,0:T(8,128)(2,1)S(1)}, bf16[2,128,16,144]{1,3,2,0:T(8,128)(2,1)S(1)}, ...), condition=%wide.region_2.3_spmd, body=%wide.region_1.2_spmd.sunk | while | flops 1409030 | bytes 2687151 | solution.py:124
  10.1 5.7 %collective-permute-start = (bf16[4,16,256]{2,1,0:T(8,128)(2,1)S(1)}, bf16[4,16,256]{2,1,0:T(8,128)(2,1)S(1)}, u32[]{:S(2)}, u32[]{:S(2)}) collective-permute-start(bf16[4,16,256]{2,1,0:T(8,128)(2,1)S(1)} %get-tuple-element.151), channel_id=1, source_target_pairs={{0,15},{1,0},{2,1},{3,2},{4,3},{5,4},{6,5},{7,6},{8,7},{9,8},{10,9... | collective-permute-start | bytes 98312 | tf_op jit(solution)/shard_map/while/body/eval_jaxpr/ppermute | solution.py:28
  15.8 1.6 %collective-permute-done = bf16[4,16,256]{2,1,0:T(8,128)(2,1)S(1)} collective-permute-done((bf16[4,16,256]{2,1,0:T(8,128)(2,1)S(1)}, bf16[4,16,256]{2,1,0:T(8,128)(2,1)S(1)}, u32[]{:S(2)}, u32[]{:S(2)}) %collective-permute-start) | collective-permute-done | bytes 32800 | tf_op jit(solution)/shard_map/while/body/eval_jaxpr/ppermute | solution.py:28
  19.8 4.5 %collective-permute-start = (bf16[4,16,256]{2,1,0:T(8,128)(2,1)S(1)}, bf16[4,16,256]{2,1,0:T(8,128)(2,1)S(1)}, u32[]{:S(2)}, u32[]{:S(2)}) collective-permute-start(bf16[4,16,256]{2,1,0:T(8,128)(2,1)S(1)} %get-tuple-element.151), channel_id=1, source_target_pairs={{0,15},{1,0},{2,1},{3,2},{4,3},{5,4},{6,5},{7,6},{8,7},{9,8},{10,9... | collective-permute-start | bytes 98312 | tf_op jit(solution)/shard_map/while/body/eval_jaxpr/ppermute | solution.py:28
  24.3 1.6 %collective-permute-done = bf16[4,16,256]{2,1,0:T(8,128)(2,1)S(1)} collective-permute-done((bf16[4,16,256]{2,1,0:T(8,128)(2,1)S(1)}, bf16[4,16,256]{2,1,0:T(8,128)(2,1)S(1)}, u32[]{:S(2)}, u32[]{:S(2)}) %collective-permute-start) | collective-permute-done | bytes 32800 | tf_op jit(solution)/shard_map/while/body/eval_jaxpr/ppermute | solution.py:28
  26.4 0.4 fusion.81
  28.2 4.5 %collective-permute-start = (bf16[4,16,256]{2,1,0:T(8,128)(2,1)S(1)}, bf16[4,16,256]{2,1,0:T(8,128)(2,1)S(1)}, u32[]{:S(2)}, u32[]{:S(2)}) collective-permute-start(bf16[4,16,256]{2,1,0:T(8,128)(2,1)S(1)} %get-tuple-element.151), channel_id=1, source_target_pairs={{0,15},{1,0},{2,1},{3,2},{4,3},{5,4},{6,5},{7,6},{8,7},{9,8},{10,9... | collective-permute-start | bytes 98312 | tf_op jit(solution)/shard_map/while/body/eval_jaxpr/ppermute | solution.py:28
  32.7 1.6 %collective-permute-done = bf16[4,16,256]{2,1,0:T(8,128)(2,1)S(1)} collective-permute-done((bf16[4,16,256]{2,1,0:T(8,128)(2,1)S(1)}, bf16[4,16,256]{2,1,0:T(8,128)(2,1)S(1)}, u32[]{:S(2)}, u32[]{:S(2)}) %collective-permute-start) | collective-permute-done | bytes 32800 | tf_op jit(solution)/shard_map/while/body/eval_jaxpr/ppermute | solution.py:28
  34.8 0.4 fusion.81
  36.6 4.5 %collective-permute-start = (bf16[4,16,256]{2,1,0:T(8,128)(2,1)S(1)}, bf16[4,16,256]{2,1,0:T(8,128)(2,1)S(1)}, u32[]{:S(2)}, u32[]{:S(2)}) collective-permute-start(bf16[4,16,256]{2,1,0:T(8,128)(2,1)S(1)} %get-tuple-element.151), channel_id=1, source_target_pairs={{0,15},{1,0},{2,1},{3,2},{4,3},{5,4},{6,5},{7,6},{8,7},{9,8},{10,9... | collective-permute-start | bytes 98312 | tf_op jit(solution)/shard_map/while/body/eval_jaxpr/ppermute | solution.py:28
  41.1 1.6 %collective-permute-done = bf16[4,16,256]{2,1,0:T(8,128)(2,1)S(1)} collective-permute-done((bf16[4,16,256]{2,1,0:T(8,128)(2,1)S(1)}, bf16[4,16,256]{2,1,0:T(8,128)(2,1)S(1)}, u32[]{:S(2)}, u32[]{:S(2)}) %collective-permute-start) | collective-permute-done | bytes 32800 | tf_op jit(solution)/shard_map/while/body/eval_jaxpr/ppermute | solution.py:28
  43.3 0.4 fusion.81
  45.0 4.5 %collective-permute-start = (bf16[4,16,256]{2,1,0:T(8,128)(2,1)S(1)}, bf16[4,16,256]{2,1,0:T(8,128)(2,1)S(1)}, u32[]{:S(2)}, u32[]{:S(2)}) collective-permute-start(bf16[4,16,256]{2,1,0:T(8,128)(2,1)S(1)} %get-tuple-element.151), channel_id=1, source_target_pairs={{0,15},{1,0},{2,1},{3,2},{4,3},{5,4},{6,5},{7,6},{8,7},{9,8},{10,9... | collective-permute-start | bytes 98312 | tf_op jit(solution)/shard_map/while/body/eval_jaxpr/ppermute | solution.py:28
  49.5 1.6 %collective-permute-done = bf16[4,16,256]{2,1,0:T(8,128)(2,1)S(1)} collective-permute-done((bf16[4,16,256]{2,1,0:T(8,128)(2,1)S(1)}, bf16[4,16,256]{2,1,0:T(8,128)(2,1)S(1)}, u32[]{:S(2)}, u32[]{:S(2)}) %collective-permute-start) | collective-permute-done | bytes 32800 | tf_op jit(solution)/shard_map/while/body/eval_jaxpr/ppermute | solution.py:28
  51.7 0.4 fusion.81
  53.4 4.5 %collective-permute-start = (bf16[4,16,256]{2,1,0:T(8,128)(2,1)S(1)}, bf16[4,16,256]{2,1,0:T(8,128)(2,1)S(1)}, u32[]{:S(2)}, u32[]{:S(2)}) collective-permute-start(bf16[4,16,256]{2,1,0:T(8,128)(2,1)S(1)} %get-tuple-element.151), channel_id=1, source_target_pairs={{0,15},{1,0},{2,1},{3,2},{4,3},{5,4},{6,5},{7,6},{8,7},{9,8},{10,9... | collective-permute-start | bytes 98312 | tf_op jit(solution)/shard_map/while/body/eval_jaxpr/ppermute | solution.py:28
  57.9 1.6 %collective-permute-done = bf16[4,16,256]{2,1,0:T(8,128)(2,1)S(1)} collective-permute-done((bf16[4,16,256]{2,1,0:T(8,128)(2,1)S(1)}, bf16[4,16,256]{2,1,0:T(8,128)(2,1)S(1)}, u32[]{:S(2)}, u32[]{:S(2)}) %collective-permute-start) | collective-permute-done | bytes 32800 | tf_op jit(solution)/shard_map/while/body/eval_jaxpr/ppermute | solution.py:28
  60.1 0.4 fusion.81
  61.9 4.5 %collective-permute-start = (bf16[4,16,256]{2,1,0:T(8,128)(2,1)S(1)}, bf16[4,16,256]{2,1,0:T(8,128)(2,1)S(1)}, u32[]{:S(2)}, u32[]{:S(2)}) collective-permute-start(bf16[4,16,256]{2,1,0:T(8,128)(2,1)S(1)} %get-tuple-element.151), channel_id=1, source_target_pairs={{0,15},{1,0},{2,1},{3,2},{4,3},{5,4},{6,5},{7,6},{8,7},{9,8},{10,9... | collective-permute-start | bytes 98312 | tf_op jit(solution)/shard_map/while/body/eval_jaxpr/ppermute | solution.py:28
  66.4 1.6 %collective-permute-done = bf16[4,16,256]{2,1,0:T(8,128)(2,1)S(1)} collective-permute-done((bf16[4,16,256]{2,1,0:T(8,128)(2,1)S(1)}, bf16[4,16,256]{2,1,0:T(8,128)(2,1)S(1)}, u32[]{:S(2)}, u32[]{:S(2)}) %collective-permute-start) | collective-permute-done | bytes 32800 | tf_op jit(solution)/shard_map/while/body/eval_jaxpr/ppermute | solution.py:28
  68.5 0.4 fusion.81
  70.3 4.5 %collective-permute-start = (bf16[4,16,256]{2,1,0:T(8,128)(2,1)S(1)}, bf16[4,16,256]{2,1,0:T(8,128)(2,1)S(1)}, u32[]{:S(2)}, u32[]{:S(2)}) collective-permute-start(bf16[4,16,256]{2,1,0:T(8,128)(2,1)S(1)} %get-tuple-element.151), channel_id=1, source_target_pairs={{0,15},{1,0},{2,1},{3,2},{4,3},{5,4},{6,5},{7,6},{8,7},{9,8},{10,9... | collective-permute-start | bytes 98312 | tf_op jit(solution)/shard_map/while/body/eval_jaxpr/ppermute | solution.py:28
  74.8 1.6 %collective-permute-done = bf16[4,16,256]{2,1,0:T(8,128)(2,1)S(1)} collective-permute-done((bf16[4,16,256]{2,1,0:T(8,128)(2,1)S(1)}, bf16[4,16,256]{2,1,0:T(8,128)(2,1)S(1)}, u32[]{:S(2)}, u32[]{:S(2)}) %collective-permute-start) | collective-permute-done | bytes 32800 | tf_op jit(solution)/shard_map/while/body/eval_jaxpr/ppermute | solution.py:28
  77.0 0.4 fusion.81
  78.7 1.3 %fusion.11 = bf16[16,64,144]{2,1,0:T(8,128)(2,1)} fusion(bf16[2,128,16,144]{1,3,2,0:T(8,128)(2,1)S(1)} %get-tuple-element.84, bf16[1,128,64]{1,2,0:T(8,128)(2,1)S(1)} %get-tuple-element.112, bf16[1,128,64]{1,2,0:T(8,128)(2,1)S(1)} %get-tuple-element.111), kind=kOutput, calls=%fused_computation.23 | convolution fusion | flops 75710464 | bytes 1507328 | tf_op jit(solution)/shard_map/pbij,pbt->itj/dot_general | solution.py:126
  (80 shorter events, 18.7 us)
Async XLA Ops:
  3.3 3.1 %collective-permute-start.1 = (bf16[4,16384]{1,0:T(4,128)(2,1)S(1)}, bf16[4,16384]{1,0:T(4,128)(2,1)S(1)}, u32[]{:S(2)}, u32[]{:S(2)}) collective-permute-start(bf16[4,16384]{1,0:T(4,128)(2,1)S(1)} %convolution_convert_fusion), channel_id=1, source_target_pairs={{0,1},{1,0},{2,3},{3,2},{4,5},{5,4},{6,7},{7,6},{8,9},{9,8},{10,11... | collective-permute-start | bytes 393224 | tf_op jit(solution)/shard_map/ppermute | solution.py:22
  10.1 7.3 %collective-permute-start = (bf16[4,16,256]{2,1,0:T(8,128)(2,1)S(1)}, bf16[4,16,256]{2,1,0:T(8,128)(2,1)S(1)}, u32[]{:S(2)}, u32[]{:S(2)}) collective-permute-start(bf16[4,16,256]{2,1,0:T(8,128)(2,1)S(1)} %get-tuple-element.151), channel_id=1, source_target_pairs={{0,15},{1,0},{2,1},{3,2},{4,3},{5,4},{6,5},{7,6},{8,7},{9,8},{10,9... | collective-permute-start | bytes 98312 | tf_op jit(solution)/shard_map/while/body/eval_jaxpr/ppermute | solution.py:28
  19.8 6.1 %collective-permute-start = (bf16[4,16,256]{2,1,0:T(8,128)(2,1)S(1)}, bf16[4,16,256]{2,1,0:T(8,128)(2,1)S(1)}, u32[]{:S(2)}, u32[]{:S(2)}) collective-permute-start(bf16[4,16,256]{2,1,0:T(8,128)(2,1)S(1)} %get-tuple-element.151), channel_id=1, source_target_pairs={{0,15},{1,0},{2,1},{3,2},{4,3},{5,4},{6,5},{7,6},{8,7},{9,8},{10,9... | collective-permute-start | bytes 98312 | tf_op jit(solution)/shard_map/while/body/eval_jaxpr/ppermute | solution.py:28
  28.2 6.1 %collective-permute-start = (bf16[4,16,256]{2,1,0:T(8,128)(2,1)S(1)}, bf16[4,16,256]{2,1,0:T(8,128)(2,1)S(1)}, u32[]{:S(2)}, u32[]{:S(2)}) collective-permute-start(bf16[4,16,256]{2,1,0:T(8,128)(2,1)S(1)} %get-tuple-element.151), channel_id=1, source_target_pairs={{0,15},{1,0},{2,1},{3,2},{4,3},{5,4},{6,5},{7,6},{8,7},{9,8},{10,9... | collective-permute-start | bytes 98312 | tf_op jit(solution)/shard_map/while/body/eval_jaxpr/ppermute | solution.py:28
  36.6 6.1 %collective-permute-start = (bf16[4,16,256]{2,1,0:T(8,128)(2,1)S(1)}, bf16[4,16,256]{2,1,0:T(8,128)(2,1)S(1)}, u32[]{:S(2)}, u32[]{:S(2)}) collective-permute-start(bf16[4,16,256]{2,1,0:T(8,128)(2,1)S(1)} %get-tuple-element.151), channel_id=1, source_target_pairs={{0,15},{1,0},{2,1},{3,2},{4,3},{5,4},{6,5},{7,6},{8,7},{9,8},{10,9... | collective-permute-start | bytes 98312 | tf_op jit(solution)/shard_map/while/body/eval_jaxpr/ppermute | solution.py:28
  45.0 6.1 %collective-permute-start = (bf16[4,16,256]{2,1,0:T(8,128)(2,1)S(1)}, bf16[4,16,256]{2,1,0:T(8,128)(2,1)S(1)}, u32[]{:S(2)}, u32[]{:S(2)}) collective-permute-start(bf16[4,16,256]{2,1,0:T(8,128)(2,1)S(1)} %get-tuple-element.151), channel_id=1, source_target_pairs={{0,15},{1,0},{2,1},{3,2},{4,3},{5,4},{6,5},{7,6},{8,7},{9,8},{10,9... | collective-permute-start | bytes 98312 | tf_op jit(solution)/shard_map/while/body/eval_jaxpr/ppermute | solution.py:28
  53.4 6.1 %collective-permute-start = (bf16[4,16,256]{2,1,0:T(8,128)(2,1)S(1)}, bf16[4,16,256]{2,1,0:T(8,128)(2,1)S(1)}, u32[]{:S(2)}, u32[]{:S(2)}) collective-permute-start(bf16[4,16,256]{2,1,0:T(8,128)(2,1)S(1)} %get-tuple-element.151), channel_id=1, source_target_pairs={{0,15},{1,0},{2,1},{3,2},{4,3},{5,4},{6,5},{7,6},{8,7},{9,8},{10,9... | collective-permute-start | bytes 98312 | tf_op jit(solution)/shard_map/while/body/eval_jaxpr/ppermute | solution.py:28
  61.9 6.1 %collective-permute-start = (bf16[4,16,256]{2,1,0:T(8,128)(2,1)S(1)}, bf16[4,16,256]{2,1,0:T(8,128)(2,1)S(1)}, u32[]{:S(2)}, u32[]{:S(2)}) collective-permute-start(bf16[4,16,256]{2,1,0:T(8,128)(2,1)S(1)} %get-tuple-element.151), channel_id=1, source_target_pairs={{0,15},{1,0},{2,1},{3,2},{4,3},{5,4},{6,5},{7,6},{8,7},{9,8},{10,9... | collective-permute-start | bytes 98312 | tf_op jit(solution)/shard_map/while/body/eval_jaxpr/ppermute | solution.py:28
  70.3 6.1 %collective-permute-start = (bf16[4,16,256]{2,1,0:T(8,128)(2,1)S(1)}, bf16[4,16,256]{2,1,0:T(8,128)(2,1)S(1)}, u32[]{:S(2)}, u32[]{:S(2)}) collective-permute-start(bf16[4,16,256]{2,1,0:T(8,128)(2,1)S(1)} %get-tuple-element.151), channel_id=1, source_target_pairs={{0,15},{1,0},{2,1},{3,2},{4,3},{5,4},{6,5},{7,6},{8,7},{9,8},{10,9... | collective-permute-start | bytes 98312 | tf_op jit(solution)/shard_map/while/body/eval_jaxpr/ppermute | solution.py:28
where the time goes:
time: 80.2 us; the launch traced here: 80 us
  starting transfers between devices  37.7 us (47%)
  matrix products  12.8 us (16%)
  waiting for transfers between devices  12.8 us (16%)
  local copies, waits for them, and re-layouts  10.9 us (14%)
  other arithmetic  5.11 us (6%)
    ppermute x8, starting transfers between devices, from_behind(): return lax.ppermute(value, axis, pairs)  37.2 us
    ppermute x8, waiting for transfers between devices, from_behind(): return lax.ppermute(value, axis, pairs)  12.8 us
    another operation x18, local copies, waits for them, and re-layouts, pair_cross(): return jnp.stack([same_part, turned]).astype(jnp.bfloat16)  7.78 us
    dot_general x9, matrix products, pair_cross(): jnp.einsum('wicb,wjcb->bij', own_split, other_split, preferred_element_ty...  3.96 us
    dot_general x9, matrix products, pair_cross(): jnp.einsum('wib,wjb->bij', own_split[:, :, 1], other_split[:, :, 0], pref...  3.47 us
    dot_general x9, matrix products, pair_cross(): jnp.einsum('wib,wjb->bij', own_split[:, :, 0], other_split[:, :, 1], pref...  3.45 us
    another operation x4, other arithmetic  2.67 us
  transfers between devices with their start and end apart: 9, of which 8 were waited for; matrix products, arithmetic and copies ran while one was open for 3% of the time, Pallas kernels for 0%

commit v1 on v0

v1 whole, which is shorter than its diff:
```python
import functools
import math

import jax
import jax.numpy as jnp
import numpy as np
from jax import lax
from jax.experimental import pallas as pl
from jax.experimental.pallas import tpu as pltpu
from jax.sharding import PartitionSpec as P

NW = 4
BANDS = 128
BAND_LO = 16
SMOOTH = 4
LAGS = 64
MESH = pl.DeviceIdType.MESH


def fourier_table(samples, bands, band_low):
    times = np.arange(samples, dtype=np.int32)
    bins = band_low + np.arange(bands, dtype=np.int32)
    phase = times[:, None] * bins[None, :] % samples
    angle = np.float32(2.0 * math.pi / samples) * phase.astype(np.float32)
    turn = np.float32(2.0 * math.pi / samples) * times.astype(np.float32)
    taper = np.float32(0.5) - np.float32(0.5) * np.cos(turn)
    rows = np.concatenate([taper[:, None] * np.cos(angle), -taper[:, None] * np.sin(angle)], axis=1)
    return rows.astype(jnp.bfloat16)


def lag_table(samples, bands, band_low, lags, windows):
    bins = band_low + np.arange(bands, dtype=np.int32)
    delays = np.arange(lags, dtype=np.int32) - lags // 2
    phase = bins[:, None] * delays[None, :] % samples
    angle = np.float32(2.0 * math.pi / samples) * phase.astype(np.float32)
    weight = np.float32(1.0 / math.sqrt(windows * bands))
    rows = np.concatenate([np.cos(angle) * weight, -np.sin(angle) * weight], axis=0)
    return np.ascontiguousarray(rows.T).astype(jnp.bfloat16)


def shifted(values, steps):
    bands = values.shape[1]
    lane = lax.broadcasted_iota(jnp.int32, values.shape, 1)
    moved = pltpu.roll(values, steps % bands, 1)
    inside = lane >= steps if steps > 0 else lane < bands + steps
    return jnp.where(inside, moved, 0.0)


def whiten(spectra):
    real_part = spectra[:, :BANDS]
    imag_part = spectra[:, BANDS:]
    power = real_part * real_part + imag_part * imag_part
    below = power + shifted(power, 1)
    below = shifted(below + shifted(below, 2), 1)
    above = power + shifted(power, -1)
    above = shifted(above + shifted(above, -2), -1)
    nearby = power + below + above
    mean = jnp.sum(power, axis=1, keepdims=True) * (1.0 / BANDS)
    level = nearby * (1.0 / (2 * SMOOTH + 1)) + 0.25 * mean + 1e-05
    factor = lax.rsqrt(level)
    return jnp.concatenate([real_part * factor, imag_part * factor], axis=1).astype(jnp.bfloat16)


def kernel(
    devices, target_ref, files_ref, transform_ref, lag_ref, out_ref,
    canon, incoming, blocks, own, cross,
    swap_send, swap_recv, ring_send, ring_recv, pass_send, pass_recv,
):
    slots, channels, samples = files_ref.shape
    chips = devices // 2
    reach = chips // 2
    half = devices // 2
    me = lax.axis_index("chan")
    chip = me // 2
    core = lax.rem(me, 2)
    partner = 2 * chip + 1 - core

    def same_core(step):
        return 2 * lax.rem(chip + step, chips) + core

    barrier = pltpu.get_barrier_semaphore()
    pl.semaphore_signal(barrier, inc=1, device_id={"chan": partner}, device_id_type=MESH)

    @pl.loop(1, chips)
    def _(step):
        pl.semaphore_signal(barrier, inc=1, device_id={"chan": same_core(step)}, device_id_type=MESH)

    pieces = []
    for item in range(2 * NW):
        value = chip * (2 * NW) + item
        slot = jnp.int32(0)
        found = jnp.int32(0)
        for q in range(slots):
            hit = target_ref[q] == value
            slot = jnp.where(hit, q, slot)
            found = jnp.where(hit, 1, found)
        block = files_ref[slot]
        pieces.append(jnp.where(found > 0, block, jnp.zeros_like(block)))
    records = jnp.concatenate(pieces, axis=0)
    spectra = jnp.dot(records, transform_ref[...], preferred_element_type=jnp.float32)
    canon[...] = whiten(spectra).reshape(canon.shape)

    pl.semaphore_wait(barrier, chips)
    swap = pltpu.make_async_remote_copy(
        src_ref=canon, dst_ref=incoming, send_sem=swap_send, recv_sem=swap_recv,
        device_id={"chan": partner}, device_id_type=MESH,
    )
    swap.start()
    swap.wait()
    blocks[pl.ds(0, 2)] = canon[...] + incoming[...]

    def ring(step):
        return pltpu.make_async_remote_copy(
            src_ref=blocks.at[core], dst_ref=blocks.at[2 * step + core],
            send_sem=ring_send.at[step - 1], recv_sem=ring_recv.at[step - 1],
            device_id={"chan": same_core(chips - step)}, device_id_type=MESH,
        )

    def handed(step):
        return pltpu.make_async_remote_copy(
            src_ref=blocks.at[2 * step + core], dst_ref=blocks.at[2 * step + core],
            send_sem=pass_send.at[step - 1], recv_sem=pass_recv.at[step - 1],
            device_id={"chan": partner}, device_id_type=MESH,
        )

    @pl.loop(0, reach)
    def _(back):
        ring(reach - back).start()

    mine = blocks[core].astype(jnp.float32)
    own[:, 0] = mine[:, :, :BANDS]
    own[:, 1] = mine[:, :, BANDS:]

    def pairs(flat):
        other = blocks[flat].astype(jnp.float32)
        real_other = [other[w, :, :BANDS] for w in range(NW)]
        imag_other = [other[w, :, BANDS:] for w in range(NW)]
        rows = pl.ds(pl.multiple_of((flat - core) * channels, channels), channels)
        for i in range(channels):
            same = None
            for w in range(NW):
                real_own = own[w, 0, pl.ds(i, 1), :]
                imag_own = own[w, 1, pl.ds(i, 1), :]
                s = real_own * real_other[w] + imag_own * imag_other[w]
                t = imag_own * real_other[w] - real_own * imag_other[w]
                same, turned = (s, t) if same is None else (same + s, turned + t)
            cross[i, rows, :] = jnp.concatenate([same, turned], axis=1).astype(jnp.bfloat16)

    pairs(core)

    @pl.when(core == 0)
    def _():
        pairs(1)

    @pl.loop(1, reach + 1)
    def _(step):
        ring(step).wait()
        handed(step).start()
        pairs(2 * step + core)

        @pl.when(step > 1)
        def _():
            handed(step - 1).wait()
            pairs(2 * (step - 1) + 1 - core)

    handed(reach).wait()

    @pl.when(core == 1)
    def _():
        pairs(2 * reach)

    for i in range(channels):
        out_ref[i] = lax.dot_general(
            lag_ref[...], cross[i], (((1,), (1,)), ((), ())), preferred_element_type=jnp.float32
        ).astype(out_ref.dtype)


def shards(file_blocks, block_target):
    slots, channels, samples = file_blocks.shape
    devices = lax.axis_size("chan")
    reach = devices // 4
    columns = (devices // 2 + 1) * channels
    transform = jnp.asarray(fourier_table(samples, BANDS, BAND_LO))
    lag_rows = jnp.asarray(lag_table(samples, BANDS, BAND_LO, LAGS, NW))
    vmem = pl.BlockSpec(memory_space=pltpu.VMEM)
    return pl.pallas_call(
        functools.partial(kernel, devices),
        out_shape=jax.ShapeDtypeStruct((channels, LAGS, columns), jnp.bfloat16),
        in_specs=[pl.BlockSpec(memory_space=pltpu.SMEM), vmem, vmem, vmem],
        out_specs=vmem,
        scratch_shapes=[
            pltpu.VMEM((2, NW, channels, 2 * BANDS), jnp.bfloat16),
            pltpu.VMEM((2, NW, channels, 2 * BANDS), jnp.bfloat16),
            pltpu.VMEM((2 * (reach + 1), NW, channels, 2 * BANDS), jnp.bfloat16),
            pltpu.VMEM((NW, 2, channels, BANDS), jnp.float32),
            pltpu.VMEM((channels, columns, 2 * BANDS), jnp.bfloat16),
            pltpu.SemaphoreType.DMA,
            pltpu.SemaphoreType.DMA,
            pltpu.SemaphoreType.DMA((reach,)),
            pltpu.SemaphoreType.DMA((reach,)),
            pltpu.SemaphoreType.DMA((reach,)),
            pltpu.SemaphoreType.DMA((reach,)),
        ],
        compiler_params=pltpu.CompilerParams(collective_id=0, has_side_effects=True),
        name="correlate",
    )(block_target, file_blocks, transform, lag_rows)


def solution(mesh):
    return jax.shard_map(
        shards,
        mesh=mesh,
        in_specs=(P(("day", "chan"), None, None), P(("day", "chan"))),
        out_specs=P(("day", "chan"), None, None),
        check_vma=False,
    )
```

time: 80.2 us -> 18 us (0.22)
  the two profiles are of different devices: /device:TPU:0 before, /device:TPU:15 now
where the time goes in v1:
time: 18 us; the launch traced here: 17.8 us
  Pallas kernels  15.9 us (88%)
  local copies, waits for them, and re-layouts  1.88 us (10%)
    pallas_call x1, Pallas kernels, shards(): pl.pallas_call(functools.partial(kernel, devices), out_shape=jax.ShapeDty...  15.9 us
    unnamed x1, local copies, waits for them, and re-layouts  1.88 us

profile of v1, /device:TPU:15, one launch (start us, length us, event | category | flops | bytes accessed | tf_op | source)
XLA Modules:
  0.0 17.8 jit_solution(17594175547560174871)
XLA Ops:
  0.0 15.9 %correlate.1 = bf16[16,64,144]{2,1,0:T(8,128)(2,1)} custom-call(s32[7]{0:T(128)} %target_ref.1, bf16[7,16,1024]{2,1,0:T(8,128)(2,1)} %files_ref.1, bf16[1024,256]{1,0:T(8,128)(2,1)} %constant.4.clone.transform_ref, bf16[64,256]{1,0:T(8,128)(2,1)} %constant.5.clone.lag_ref), custom_call_target="tpu_custom_call" | custom-call | tf_op jit(solution)/shard_map/correlate/pallas_call | solution.py:186
  15.9 1.9 %copy.6 = bf16[16,64,144]{2,1,0:T(8,128)(2,1)} copy(bf16[16,64,144]{2,1,0:T(8,128)(2,1)} %correlate.1) | data formatting | bytes 589824

commit v2 on v1

--- a/solution.py
+++ b/solution.py
@@ -62,9 +62,9 @@
 
 
 def kernel(
-    devices, target_ref, files_ref, transform_ref, lag_ref, out_ref,
-    canon, incoming, blocks, own, cross,
-    swap_send, swap_recv, ring_send, ring_recv, pass_send, pass_recv,
+    devices, target_hbm, files_hbm, transform_hbm, lag_hbm, out_ref,
+    target_ref, files_ref, transform_ref, lag_ref, canon, incoming, blocks, own, cross,
+    load_sems, swap_send, swap_recv, ring_send, ring_recv, pass_send, pass_recv,
 ):
     slots, channels, samples = files_ref.shape
     chips = devices // 2
@@ -84,6 +84,18 @@
     @pl.loop(1, chips)
     def _(step):
         pl.semaphore_signal(barrier, inc=1, device_id={"chan": same_core(step)}, device_id_type=MESH)
+
+    loads = [
+        pltpu.make_async_copy(source, target, load_sems.at[index])
+        for index, (source, target) in enumerate([
+            (target_hbm, target_ref), (files_hbm, files_ref),
+            (transform_hbm, transform_ref), (lag_hbm, lag_ref),
+        ])
+    ]
+    for load in loads:
+        load.start()
+    for load in loads:
+        load.wait()
 
     pieces = []
     for item in range(2 * NW):
@@ -152,27 +164,32 @@
     def _():
         pairs(1)
 
-    @pl.loop(1, reach + 1)
+    def lagged(first, count):
+        for i in range(channels):
+            out_ref[i, :, pl.ds(first, count)] = lax.dot_general(
+                lag_ref[...], cross[i, pl.ds(first, count), :], (((1,), (1,)), ((), ())),
+                preferred_element_type=jnp.float32,
+            ).astype(out_ref.dtype)
+
+    def take_handed(step):
+        handed(step).wait()
+        pairs(2 * step + 1 - core)
+
+    @pl.loop(1, reach)
     def _(step):
         ring(step).wait()
         handed(step).start()
         pairs(2 * step + core)
-
-        @pl.when(step > 1)
-        def _():
-            handed(step - 1).wait()
-            pairs(2 * (step - 1) + 1 - core)
-
+        pl.when(step > 1)(lambda: take_handed(step - 1))
+
+    take_handed(reach - 1)
+    ring(reach).wait()
+    handed(reach).start()
+    pairs(2 * reach + core)
+    lagged(half * channels, channels)
     handed(reach).wait()
-
-    @pl.when(core == 1)
-    def _():
-        pairs(2 * reach)
-
-    for i in range(channels):
-        out_ref[i] = lax.dot_general(
-            lag_ref[...], cross[i], (((1,), (1,)), ((), ())), preferred_element_type=jnp.float32
-        ).astype(out_ref.dtype)
+    pl.when(core == 1)(lambda: pairs(2 * reach))
+    lagged(0, half * channels)
 
 
 def shards(file_blocks, block_target):
@@ -182,18 +199,24 @@
     columns = (devices // 2 + 1) * channels
     transform = jnp.asarray(fourier_table(samples, BANDS, BAND_LO))
     lag_rows = jnp.asarray(lag_table(samples, BANDS, BAND_LO, LAGS, NW))
-    vmem = pl.BlockSpec(memory_space=pltpu.VMEM)
+    hbm = pl.BlockSpec(memory_space=pltpu.HBM)
+    vmem_bytes = 2 * columns * channels * 2 * BANDS * 2 + (12 << 20)
     return pl.pallas_call(
         functools.partial(kernel, devices),
         out_shape=jax.ShapeDtypeStruct((channels, LAGS, columns), jnp.bfloat16),
-        in_specs=[pl.BlockSpec(memory_space=pltpu.SMEM), vmem, vmem, vmem],
-        out_specs=vmem,
+        in_specs=[hbm, hbm, hbm, hbm],
+        out_specs=pl.BlockSpec(memory_space=pltpu.VMEM),
         scratch_shapes=[
+            pltpu.SMEM(block_target.shape, jnp.int32),
+            pltpu.VMEM(file_blocks.shape, jnp.bfloat16),
+            pltpu.VMEM(transform.shape, jnp.bfloat16),
+            pltpu.VMEM(lag_rows.shape, jnp.bfloat16),
             pltpu.VMEM((2, NW, channels, 2 * BANDS), jnp.bfloat16),
             pltpu.VMEM((2, NW, channels, 2 * BANDS), jnp.bfloat16),
             pltpu.VMEM((2 * (reach + 1), NW, channels, 2 * BANDS), jnp.bfloat16),
             pltpu.VMEM((NW, 2, channels, BANDS), jnp.float32),
             pltpu.VMEM((channels, columns, 2 * BANDS), jnp.bfloat16),
+            pltpu.SemaphoreType.DMA((4,)),
             pltpu.SemaphoreType.DMA,
             pltpu.SemaphoreType.DMA,
             pltpu.SemaphoreType.DMA((reach,)),
@@ -201,9 +224,14 @@
             pltpu.SemaphoreType.DMA((reach,)),
             pltpu.SemaphoreType.DMA((reach,)),
         ],
-        compiler_params=pltpu.CompilerParams(collective_id=0, has_side_effects=True),
+        compiler_params=pltpu.CompilerParams(
+            collective_id=0, has_side_effects=True, vmem_limit_bytes=vmem_bytes
+        ),
         name="correlate",
-    )(block_target, file_blocks, transform, lag_rows)
+    )(*[
+        pltpu.with_memory_space_constraint(value, pltpu.HBM)
+        for value in (block_target, file_blocks, transform, lag_rows)
+    ])
 
 
 def solution(mesh):

time: 18 us -> 15.7 us (0.87)
  Pallas kernels: 15.9 us -> 14.8 us
  local copies, waits for them, and re-layouts: 1.88 us -> 0.8 us
    pallas_call x1, Pallas kernels: 15.9 us -> 14.8 us  [shards(): pl.pallas_call(functools.partial(kernel, devices), out_shape=jax.ShapeDty...]
    unnamed x1, local copies, waits for them, and re-layouts: 1.88 us -> 0.8 us
where the time goes in v2:
time: 15.7 us; the launch traced here: 15.6 us
  Pallas kernels  14.8 us (94%)
  local copies, waits for them, and re-layouts  0.8 us (5%)
    pallas_call x1, Pallas kernels, shards(): pl.pallas_call(functools.partial(kernel, devices), out_shape=jax.ShapeDty...  14.8 us
    unnamed x1, local copies, waits for them, and re-layouts  0.8 us

profile of v2, /device:TPU:15, one launch (start us, length us, event | category | flops | bytes accessed | tf_op | source)
XLA Modules:
  0.0 15.6 jit_solution(11348872259889022922)
XLA Ops:
  0.0 14.8 %correlate.1 = bf16[16,64,144]{2,1,0:T(8,128)(2,1)S(1)} custom-call(s32[7]{0:T(128)} %target_hbm.1, bf16[7,16,1024]{2,1,0:T(8,128)(2,1)} %files_hbm.1, bf16[1024,256]{1,0:T(8,128)(2,1)} %constant.4.clone.transform_hbm, bf16[64,256]{1,0:T(8,128)(2,1)} %constant.5.clone.lag_hbm), custom_call_target="tpu_custom_call" | custom-call | tf_op jit(solution)/shard_map/correlate/pallas_call | solution.py:204
  14.8 0.8 %copy.6 = bf16[16,64,144]{2,1,0:T(8,128)(2,1)} copy(bf16[16,64,144]{2,1,0:T(8,128)(2,1)S(1)} %correlate.1) | data formatting | bytes 589824

commit v3 on v2

--- a/solution.py
+++ b/solution.py
@@ -64,7 +64,7 @@
 def kernel(
     devices, target_hbm, files_hbm, transform_hbm, lag_hbm, out_ref,
     target_ref, files_ref, transform_ref, lag_ref, canon, incoming, blocks, own, cross,
-    load_sems, swap_send, swap_recv, ring_send, ring_recv, pass_send, pass_recv,
+    pair_sem, all_sem, load_sems, swap_send, swap_recv, ring_send, ring_recv, pass_send, pass_recv,
 ):
     slots, channels, samples = files_ref.shape
     chips = devices // 2
@@ -78,12 +78,14 @@
     def same_core(step):
         return 2 * lax.rem(chip + step, chips) + core
 
+    def other_core(step):
+        return 2 * lax.rem(chip + step, chips) + 1 - core
+
     barrier = pltpu.get_barrier_semaphore()
-    pl.semaphore_signal(barrier, inc=1, device_id={"chan": partner}, device_id_type=MESH)
-
-    @pl.loop(1, chips)
-    def _(step):
-        pl.semaphore_signal(barrier, inc=1, device_id={"chan": same_core(step)}, device_id_type=MESH)
+
+    @pl.when(core == 1)
+    def _():
+        pl.semaphore_signal(barrier, inc=1, device_id={"chan": partner}, device_id_type=MESH)
 
     loads = [
         pltpu.make_async_copy(source, target, load_sems.at[index])
@@ -94,6 +96,20 @@
     ]
     for load in loads:
         load.start()
+
+    @pl.when(core == 0)
+    def _():
+        pl.semaphore_wait(barrier, 1)
+        pl.semaphore_signal(pair_sem, inc=1, device_id={"chan": partner}, device_id_type=MESH)
+
+    @pl.when(core == 1)
+    def _():
+        pl.semaphore_wait(pair_sem, 1)
+
+        @pl.loop(1, chips)
+        def _(step):
+            pl.semaphore_signal(barrier, inc=1, device_id={"chan": same_core(step)}, device_id_type=MESH)
+
     for load in loads:
         load.wait()
 
@@ -112,7 +128,6 @@
     spectra = jnp.dot(records, transform_ref[...], preferred_element_type=jnp.float32)
     canon[...] = whiten(spectra).reshape(canon.shape)
 
-    pl.semaphore_wait(barrier, chips)
     swap = pltpu.make_async_remote_copy(
         src_ref=canon, dst_ref=incoming, send_sem=swap_send, recv_sem=swap_recv,
         device_id={"chan": partner}, device_id_type=MESH,
@@ -121,6 +136,15 @@
     swap.wait()
     blocks[pl.ds(0, 2)] = canon[...] + incoming[...]
 
+    @pl.when(core == 1)
+    def _():
+        pl.semaphore_wait(barrier, chips - 1)
+        pl.semaphore_signal(all_sem, inc=1, device_id={"chan": partner}, device_id_type=MESH)
+
+    @pl.when(core == 0)
+    def _():
+        pl.semaphore_wait(all_sem, 1)
+
     def ring(step):
         return pltpu.make_async_remote_copy(
             src_ref=blocks.at[core], dst_ref=blocks.at[2 * step + core],
@@ -135,9 +159,15 @@
             device_id={"chan": partner}, device_id_type=MESH,
         )
 
-    @pl.loop(0, reach)
-    def _(back):
-        ring(reach - back).start()
+    def direct(step):
+        return pltpu.make_async_remote_copy(
+            src_ref=blocks.at[core], dst_ref=blocks.at[2 * step + core],
+            send_sem=pass_send.at[step - 1], recv_sem=pass_recv.at[step - 1],
+            device_id={"chan": other_core(chips - step)}, device_id_type=MESH,
+        )
+
+    pl.loop(1, reach + 1)(lambda step: ring(step).start())
+    pl.when(core == 0)(lambda: direct(reach).start())
 
     mine = blocks[core].astype(jnp.float32)
     own[:, 0] = mine[:, :, :BANDS]
@@ -183,13 +213,17 @@
         pl.when(step > 1)(lambda: take_handed(step - 1))
 
     take_handed(reach - 1)
+    lagged(0, (half - 1) * channels)
     ring(reach).wait()
-    handed(reach).start()
     pairs(2 * reach + core)
-    lagged(half * channels, channels)
-    handed(reach).wait()
-    pl.when(core == 1)(lambda: pairs(2 * reach))
-    lagged(0, half * channels)
+    pl.when(core == 0)(lambda: direct(reach).wait_send())
+
+    @pl.when(core == 1)
+    def _():
+        handed(reach).wait_recv()
+        pairs(2 * reach)
+
+    lagged((half - 1) * channels, 2 * channels)
 
 
 def shards(file_blocks, block_target):
@@ -216,6 +250,8 @@
             pltpu.VMEM((2 * (reach + 1), NW, channels, 2 * BANDS), jnp.bfloat16),
             pltpu.VMEM((NW, 2, channels, BANDS), jnp.float32),
             pltpu.VMEM((channels, columns, 2 * BANDS), jnp.bfloat16),
+            pltpu.SemaphoreType.REGULAR,
+            pltpu.SemaphoreType.REGULAR,
             pltpu.SemaphoreType.DMA((4,)),
             pltpu.SemaphoreType.DMA,
             pltpu.SemaphoreType.DMA,

time: 15.7 us -> 14.3 us (0.911)
  the two profiles are of different devices: /device:TPU:15 before, /device:TPU:0 now
where the time goes in v3:
time: 14.3 us; the launch traced here: 14.1 us
  Pallas kernels  13.3 us (93%)
  local copies, waits for them, and re-layouts  0.8 us (6%)
    pallas_call x1, Pallas kernels, shards(): pl.pallas_call(functools.partial(kernel, devices), out_shape=jax.ShapeDty...  13.3 us
    unnamed x1, local copies, waits for them, and re-layouts  0.8 us

profile of v3, /device:TPU:0, one launch (start us, length us, event | category | flops | bytes accessed | tf_op | source)
XLA Modules:
  0.0 14.1 jit_solution(1392403308904295300)
XLA Ops:
  0.0 13.3 %correlate.1 = bf16[16,64,144]{2,1,0:T(8,128)(2,1)S(1)} custom-call(s32[7]{0:T(128)} %target_hbm.1, bf16[7,16,1024]{2,1,0:T(8,128)(2,1)} %files_hbm.1, bf16[1024,256]{1,0:T(8,128)(2,1)} %constant.4.clone.transform_hbm, bf16[64,256]{1,0:T(8,128)(2,1)} %constant.5.clone.lag_hbm), custom_call_target="tpu_custom_call" | custom-call | tf_op jit(solution)/shard_map/correlate/pallas_call | solution.py:238
  13.3 0.8 %copy.6 = bf16[16,64,144]{2,1,0:T(8,128)(2,1)} copy(bf16[16,64,144]{2,1,0:T(8,128)(2,1)S(1)} %correlate.1) | data formatting | bytes 589824
